TPU v7x, 32 devices: a whole 2x2x4 slice. The times are simulated.
32 devices in a mesh: groups: 2 (over y), tp: 4 (over z), seq: 4 (over x, core).
Axes of the slice: x: 2, y: 2, z: 4, core: 2. Of those that a mesh axis runs over, the one named last changes fastest.
Arguments:
- kv_prefill: bfloat16 [2, 2, 8, 32768, 128], P(None, None, 'groups', ('tp', 'seq')), parts along dimension 2, may hold values from -10 to 10
- queries: bfloat16 [2, 8, 64, 128], P(None, ('groups', 'seq'), 'tp'), parts along dimension 1, may hold values from -512 to 512
- new_kv: bfloat16 [2, 2, 8, 8, 128], P(None, None, ('groups', 'seq')), parts along dimension 2, may hold values from -4.5 to 4.5
- lengths: int32 [8], P(('groups', 'seq')), parts along dimension 0, may hold values from 2048 to 4095
- page_slots: int32 [8, 256], P(('groups', 'seq')), parts along dimension 0, may hold values from 0 to 255, each once within a row
Outputs:
- decode_pool: bfloat16 [2, 2, 8, 2048, 16, 128], P(None, None, 'tp', ('groups', 'seq')), parts along dimension 3
- attention_out: bfloat16 [2, 8, 64, 128], P(None, ('groups', 'seq'), 'tp'), parts along dimension 1
There are 2 independent parts, one for each index of `groups`. A program takes and returns all parts, laid end to end along the dimension named above; each array names one. Nothing has to cross between parts.
Inputs may be any that keep to these rules, and one draw needn't show every extreme that they name: Row b belongs to sequence b: its page j goes to slot page_slots[b, j] of the row's block of 256 slots; each row uses every slot once.
All inputs are finite; a program needn't handle non-finite values.
Results may differ from a plain program's by a relative error of at most 0.01.
Values may be sent and summed in bfloat16 or wider, within the bound.
No kernel may reach another device: no remote copies, remote signals or barrier semaphores. Data moves between devices by JAX's collectives and lax.ppermute only.
A program may use at most 64 MiB of HBM per device.

v0:
```python
import functools
import math

import jax
import jax.numpy as jnp
from jax import lax
from jax.experimental import pallas as pl
from jax.experimental.pallas import tpu as pltpu
from jax.sharding import PartitionSpec as P


KVH = 8
PAGE = 16
CTX = 4096
TAIL = 32


def swapped(array, axis, bit):
    return lax.ppermute(array, axis, [(i, i ^ 1 << bit) for i in range(lax.axis_size(axis))])


def spread_heads(blocks, axis_dim):
    tp_ranks = lax.axis_size("tp")
    kv_rank = max(1, KVH // tp_ranks)
    fanout = tp_ranks * kv_rank // KVH
    levels = fanout.bit_length() - 1
    ordering = list(range(levels))
    my_rank = lax.axis_index("tp")
    finished = []
    for bit_index in ordering:
        partner = swapped(blocks, "tp", bit_index)
        lower_side = my_rank // (1 << bit_index) % 2 == 0
        lower_part = jnp.where(lower_side, blocks, partner)
        upper_part = jnp.where(lower_side, partner, blocks)
        higher_bits = sum((1 for earlier in finished if earlier > bit_index))
        shape_now = blocks.shape
        outer_count = 2**higher_bits
        split_shape = (
            shape_now[:axis_dim]
            + (outer_count, shape_now[axis_dim] // outer_count)
            + shape_now[axis_dim + 1 :]
        )
        paired = jnp.stack(
            (lower_part.reshape(split_shape), upper_part.reshape(split_shape)), axis=axis_dim + 1
        )
        blocks = paired.reshape(
            shape_now[:axis_dim] + (2 * shape_now[axis_dim],) + shape_now[axis_dim + 1 :]
        )
        finished.append(bit_index)
    return blocks


def repack(grouped, page_row, local_seqs):
    layers_here = grouped.shape[1]
    head_count = grouped.shape[3] // CTX
    head_dim = grouped.shape[4]
    paged_rows = grouped.reshape(
        2, layers_here, local_seqs, head_count, CTX // PAGE, PAGE, head_dim
    )
    paged_rows = paged_rows.transpose(0, 1, 3, 2, 4, 5, 6).reshape(
        2, layers_here, head_count, local_seqs * (CTX // PAGE), PAGE, head_dim
    )
    inverse = jnp.argsort(page_row)
    return jnp.take(paged_rows, inverse, axis=3)


def gathered(kv_prefill, queries, new_kv, lengths, page_slots):
    local_seqs = lengths.shape[0]
    page_row = page_slots[0]
    tp_ranks = lax.axis_size("tp")
    kv_rank = max(1, KVH // tp_ranks)
    layer_count = kv_prefill.shape[1]
    grouped = spread_heads(kv_prefill, 3)
    block_rows = kv_prefill.shape[3]
    fanout = grouped.shape[3] // block_rows
    shaped = grouped.reshape(
        2, layer_count, grouped.shape[2], fanout, 1, block_rows, grouped.shape[4]
    )
    pieces = lax.all_to_all(shaped, "seq", split_axis=2, concat_axis=4, tiled=True)
    flattened = pieces.reshape(
        2,
        pieces.shape[1],
        pieces.shape[2],
        pieces.shape[3] * pieces.shape[4] * pieces.shape[5],
        pieces.shape[6],
    )
    decode_pool = repack(flattened, page_row, local_seqs)
    first_head = lax.axis_index("tp") * KVH // tp_ranks
    fresh_rows = lax.dynamic_slice_in_dim(new_kv, first_head, kv_rank, 3)
    pages_per = CTX // PAGE
    length_now = lengths[0]
    slot_now = lax.dynamic_index_in_dim(page_row, 0 + length_now // PAGE, 0, False)
    update = fresh_rows[:, :, 0][:, :, :, None, None, :]
    decode_pool = lax.dynamic_update_slice(
        decode_pool, update, (0, 0, 0, slot_now, length_now % PAGE, 0)
    )
    slot_table = page_row.reshape(local_seqs, pages_per)
    head_dim = queries.shape[3]
    key_cache = jnp.take(decode_pool[0], slot_table, axis=2).reshape(
        layer_count, kv_rank, local_seqs, CTX, head_dim
    )
    values = jnp.take(decode_pool[1], slot_table, axis=2).reshape(
        layer_count, kv_rank, local_seqs, CTX, head_dim
    )
    grouped_q = queries.reshape(
        layer_count, local_seqs, kv_rank, queries.shape[2] // kv_rank, head_dim
    )
    scores = jnp.einsum(
        "lskgd,lkstd->lskgt", grouped_q, key_cache, preferred_element_type=jnp.float32
    ) * (1.0 / math.sqrt(head_dim))
    positions = jnp.arange(CTX, dtype=jnp.int32)
    visible = (positions[None, :] <= lengths[:, None])[None, :, None, None, :]
    masked = jnp.where(visible, scores, -1e30)
    highest = jnp.max(masked, axis=-1, keepdims=True)
    exponent = jnp.where(visible, jnp.exp(masked - highest), 0.0)
    weights = (exponent / jnp.sum(exponent, axis=-1, keepdims=True)).astype(jnp.bfloat16)
    mixed_out = jnp.einsum(
        "lskgt,lkstd->lskgd", weights, values, preferred_element_type=jnp.float32
    )
    attention_out = mixed_out.astype(jnp.bfloat16).reshape(queries.shape)
    return (decode_pool, attention_out)


def scatter_pages(slots, pieces, pool_ref, bases):
    for piece, base in zip(pieces, bases):
        kinds, pages = piece.shape[0], piece.shape[1]

        def move(j, carry):
            slot = slots[base + j]
            for k in range(kinds):
                pool_ref[k, slot] = piece[k, j]
            return carry

        lax.fori_loop(0, pages, move, 0, unroll=16)


def patch(slots, length, pool_ref, fresh):
    slot = slots[length // PAGE]
    for k in range(fresh.shape[0]):
        page = pool_ref[k, slot]
        row = lax.broadcasted_iota(jnp.int32, page.shape, 0)
        token = jnp.broadcast_to(fresh[k].astype(jnp.float32), page.shape)
        page = jnp.where(row == length % PAGE, token, page.astype(jnp.float32))
        pool_ref[k, slot] = page.astype(pool_ref.dtype)


def probabilities(q, keys, bases, length, fresh_key):
    scale = 1.0 / math.sqrt(q.shape[-1])
    new_score = jnp.sum(
        q.astype(jnp.float32) * fresh_key.astype(jnp.float32), axis=-1, keepdims=True
    ) * scale
    scores = []
    highest = new_score
    for key, base in zip(keys, bases):
        part = lax.dot_general(
            q, key, (((1,), (1,)), ((), ())), preferred_element_type=jnp.float32
        ) * scale
        position = base * PAGE + lax.broadcasted_iota(jnp.int32, part.shape, 1)
        part = jnp.where(position < length, part, -1e30)
        scores.append(part)
        highest = jnp.maximum(highest, jnp.max(part, axis=-1, keepdims=True))
    grown = [jnp.exp(part - highest) for part in scores]
    new_grown = jnp.exp(new_score - highest)
    total = new_grown
    for part in grown:
        total = total + jnp.sum(part, axis=-1, keepdims=True)
    inverse = 1.0 / total
    probs = [(part * inverse).astype(jnp.bfloat16) for part in grown]
    return probs, (new_grown * inverse).astype(jnp.bfloat16).astype(jnp.float32)


def mixed(probs, new_prob, values, fresh_value):
    out = new_prob * fresh_value.astype(jnp.float32)
    for prob, value in zip(probs, values):
        out = out + lax.dot_general(
            prob, value, (((1,), (0,)), ((), ())), preferred_element_type=jnp.float32
        )
    return out


def rows_of(piece):
    return piece.reshape(piece.shape[0] * piece.shape[1], piece.shape[2])


def head_rows(out, head, kept, heads):
    row = lax.broadcasted_iota(jnp.int32, out.shape, 0)
    mine = row // (out.shape[0] // heads) == head
    return jnp.where(mine, out, kept)


def own_kernel(parts, heads, slots, meta, own, *refs):
    others = refs[: parts - 1]
    q_ref, fresh_ref, pool_ref, out_ref = refs[parts - 1 :]
    length, head, rank_part = meta[0], meta[1], meta[2]
    pages = own.shape[3]
    bases = [(rank_part ^ e) * pages for e in range(parts)]
    pieces = [own.at[:, 0, 0]] + [other.at[:, 0] for other in others]
    pool = pool_ref.at[:, 0, 0]
    scatter_pages(slots, pieces, pool, bases)
    fresh = fresh_ref[:, 0, 0]
    patch(slots, length, pool, fresh)
    q = q_ref[0, 0]
    probs, new_prob = probabilities(
        q, [rows_of(piece[0]) for piece in pieces], bases, length, fresh[0]
    )
    out = mixed(probs, new_prob, [rows_of(piece[1]) for piece in pieces], fresh[1])
    out_ref[0, 0] = head_rows(out, head, jnp.zeros_like(out), heads).astype(out_ref.dtype)


def far_key_kernel(parts, slots, meta, *refs):
    pieces = refs[:parts]
    q_ref, fresh_ref, _, pool_ref, prob_ref, new_ref = refs[parts:]
    length, rank_part = meta[0], meta[2]
    pages = pieces[0].shape[1]
    bases = [(rank_part ^ e) * pages for e in range(parts)]
    pool = pool_ref.at[:, 0, 0]
    scatter_pages(slots, pieces, pool, bases)
    fresh = fresh_ref[:, 0, 0]
    patch(slots, length, pool, fresh)
    probs, new_prob = probabilities(
        q_ref[0, 0], [rows_of(piece[0]) for piece in pieces], bases, length, fresh[0]
    )
    for e, prob in enumerate(probs):
        prob_ref[e] = prob
    new_ref[...] = jnp.broadcast_to(new_prob, new_ref.shape)


def far_value_kernel(parts, heads, slots, meta, *refs):
    pieces = refs[:parts]
    prob_ref, new_ref, fresh_ref, kept_ref, _, pool_ref, out_ref = refs[parts:]
    length, head, rank_part = meta[0], meta[1], meta[2]
    pages = pieces[0].shape[1]
    bases = [(rank_part ^ e) * pages for e in range(parts)]
    pool = pool_ref.at[:, 0, 0]
    scatter_pages(slots, pieces, pool, bases)
    fresh = fresh_ref[:, 0, 0]
    patch(slots, length, pool, fresh)
    values = [rows_of(piece[0]) for piece in pieces]
    out = mixed([prob_ref[e] for e in range(parts)], new_ref[...], values, fresh[0])
    kept = kept_ref[0, 0].astype(jnp.float32)
    out_ref[0, 0] = head_rows(out, head, kept, heads).astype(out_ref.dtype)


def block_kernel(parts, heads, layer, slots, meta, *refs):
    pieces = refs[:parts]
    prob_ref, new_ref, fresh_ref, kept_ref = refs[parts : parts + 4]
    block_ref, sum_ref, token_ref, rest_ref = refs[2 * parts + 4 :]
    length, head, rank_part = meta[0], meta[1], meta[2]
    kind = fresh_ref.shape[0] - 1
    pages = prob_ref.shape[2] // PAGE
    bases = [(rank_part ^ e) * pages for e in range(parts)]
    scatter_pages(slots, pieces, block_ref, bases)
    fresh = fresh_ref[kind, layer, head]
    patch(slots, length, block_ref, fresh[None])
    values = [rows_of(piece[0]) for piece in pieces]
    out = mixed(
        [prob_ref[e, :, : values[e].shape[0]] for e in range(parts)],
        new_ref[...],
        values,
        fresh,
    )
    kept = kept_ref[layer, 0].astype(jnp.float32)
    sum_ref[...] = head_rows(out, head, kept, heads)
    token_ref[...] = fresh.astype(jnp.float32)
    rest_ref[...] = prob_ref[parts - 1, :, values[-1].shape[0] :]


def tail_kernel(
    parts, heads, layer, pages, slots, meta, piece, _block, sums, token, rest, _pool, _out,
    _piece, block, _sums, _token, _rest, pool, out, row_store, sems,
):
    length, head, rank_part = meta[0], meta[1], meta[2]
    kind = pool.shape[0] - 1
    tail_pages = piece.shape[1]
    slot_count = block.shape[1]
    base = (rank_part ^ (parts - 1)) * pages + pages - tail_pages
    scatter_pages(slots, [piece], block, [base])
    patch(slots, length, block, token[...][None])
    cuts = sems.shape[0] - 1
    size = slot_count // cuts
    stores = [
        pltpu.make_async_copy(
            block.at[0, pl.ds(i * size, size)],
            pool.at[kind, layer, head, pl.ds(i * size, size)],
            sems.at[i],
        )
        for i in range(cuts)
    ]
    for store in stores:
        store.start()
    share = lax.dot_general(
        rest[...], rows_of(piece[0]), (((1,), (0,)), ((), ())),
        preferred_element_type=jnp.float32,
    )
    done = sums[...]
    row_store[...] = head_rows(done + share, head, done, heads).astype(row_store.dtype)
    store = pltpu.make_async_copy(row_store, out.at[layer, 0], sems.at[cuts])
    store.start()
    store.wait()
    for store in stores:
        store.wait()


def cut_kernel(starts, src, *refs):
    outs, sems = refs[:-1], refs[-1]
    me = lax.axis_index("seq")
    copies = []
    for i, (distance, kind, layer, page) in enumerate(starts):
        kinds, layers, pages = outs[i].shape[0], outs[i].shape[1], outs[i].shape[2]
        for k in range(kinds):
            for l in range(layers):
                copies.append(
                    pltpu.make_async_copy(
                        src.at[kind + k, layer + l, me ^ distance, pl.ds(page, pages)],
                        outs[i].at[k, l],
                        sems.at[len(copies)],
                    )
                )
    for copy in copies:
        copy.start()
    for copy in copies:
        copy.wait()


def streamed(kv_prefill, queries, new_kv, lengths, page_slots):
    ranks = lax.axis_size("seq")
    me = lax.axis_index("seq")
    kinds, layers, seqs, block_rows, dim = kv_prefill.shape
    parts = CTX // block_rows
    heads = ranks // parts
    pages = block_rows // PAGE
    slot_count = page_slots.shape[1]
    q_rows = queries.shape[2]
    slots = page_slots[0]
    my_head, my_part = me // parts, me % parts
    first_head = lax.axis_index("tp") * heads
    fresh = lax.dynamic_slice_in_dim(new_kv, first_head, heads, 3)
    fresh = fresh.reshape(kinds, layers, heads, 1, dim)
    paged = kv_prefill.reshape(kinds, layers, seqs, pages, PAGE, dim)

    tail_pages = pages * TAIL // 128
    hbm_spec = pl.BlockSpec(memory_space=pl.ANY)
    vmem_spec = pl.BlockSpec(memory_space=pltpu.VMEM)
    smem_spec = pl.BlockSpec(memory_space=pltpu.SMEM)

    def cut(wanted, near_core):
        shapes = [entry[4:] + (PAGE, dim) for entry in wanted]
        return pl.pallas_call(
            functools.partial(cut_kernel, [entry[:4] for entry in wanted]),
            in_specs=[hbm_spec],
            out_specs=[vmem_spec if near_core else hbm_spec] * len(wanted),
            out_shape=[
                pltpu.VMEM(shape, kv_prefill.dtype)
                if near_core
                else jax.ShapeDtypeStruct(shape, kv_prefill.dtype)
                for shape in shapes
            ],
            scratch_shapes=[pltpu.SemaphoreType.DMA((sum(s[0] * s[1] for s in shapes),))],
            name="cut",
        )(paged)

    final = (kinds - 1, layers - 1, heads - 1)
    wanted = {}
    for kind in range(kinds):
        for layer in range(layers):
            for group in range(1, heads):
                for e in range(parts):
                    short = (kind, layer, group) == final and e == parts - 1
                    wanted["far", kind, layer, group, e] = (
                        group * parts + e, kind, layer, 0, 1, 1, pages - tail_pages * short,
                    )
                if (kind, layer, group) == (0, 0, 1):
                    for e in range(1, parts):
                        wanted["near", e] = (e, 0, 0, 0, kinds, layers, pages)
    wanted["tail"] = (
        ranks - 1, kinds - 1, layers - 1, pages - tail_pages, 1, 1, tail_pages,
    )
    entries = list(wanted.values())
    cuts = cut(entries[:1], True)
    cuts = list(cuts) + list(cut(entries[1:], False))
    received = {}
    for i, (key, entry) in enumerate(wanted.items()):
        pairs = [(r, r ^ entry[0]) for r in range(ranks)]
        received[key] = lax.ppermute(cuts[i], "seq", pairs)
    near = [received["near", e] for e in range(1, parts)]
    far = {
        key[1:4]: [received[("far",) + key[1:4] + (e,)][0] for e in range(parts)]
        for key in wanted
        if key[0] == "far"
    }
    tail = received["tail"][0]

    pool_shape = jax.ShapeDtypeStruct((kinds, layers, heads, slot_count, PAGE, dim), kv_prefill.dtype)
    out_shape = jax.ShapeDtypeStruct(queries.shape, queries.dtype)
    meta = jnp.stack([lengths[0], my_head, my_part, me]).astype(jnp.int32)
    pool, out = pl.pallas_call(
        functools.partial(own_kernel, parts, heads),
        grid_spec=pltpu.PrefetchScalarGridSpec(
            num_scalar_prefetch=2,
            grid=(layers,),
            in_specs=[
                pl.BlockSpec((kinds, 1, 1, pages, PAGE, dim), lambda l, s, m: (0, l, m[3], 0, 0, 0))
            ]
            + [
                pl.BlockSpec((kinds, 1, pages, PAGE, dim), lambda l, s, m: (0, l, 0, 0, 0))
                for _ in near
            ]
            + [
                pl.BlockSpec((1, 1, q_rows, dim), lambda l, s, m: (l, 0, 0, 0)),
                pl.BlockSpec((kinds, 1, 1, 1, dim), lambda l, s, m: (0, l, m[1], 0, 0)),
            ],
            out_specs=[
                pl.BlockSpec(
                    (kinds, 1, 1, slot_count, PAGE, dim), lambda l, s, m: (0, l, m[1], 0, 0, 0)
                ),
                pl.BlockSpec((1, 1, q_rows, dim), lambda l, s, m: (l, 0, 0, 0)),
            ],
        ),
        out_shape=(pool_shape, out_shape),
        name="own_head",
    )(slots, meta, paged, *near, queries, fresh)

    def piece_specs(pieces):
        return [pl.BlockSpec(piece.shape, lambda i, s, m: (0, 0, 0, 0)) for piece in pieces]

    weights = {}
    for kind in range(kinds):
        for layer in range(layers):
            for group in range(1, heads):
                meta = jnp.stack([lengths[0], my_head ^ group, my_part, me]).astype(jnp.int32)
                pieces = far[kind, layer, group]
                fresh_spec = pl.BlockSpec(
                    (1, 1, 1, 1, dim), lambda i, s, m, k=kind, l=layer: (k, l, m[1], 0, 0)
                )
                pool_spec = pl.BlockSpec(
                    (1, 1, 1, slot_count, PAGE, dim),
                    lambda i, s, m, k=kind, l=layer: (k, l, m[1], 0, 0, 0),
                )
                row_spec = pl.BlockSpec(
                    (1, 1, q_rows, dim), lambda i, s, m, l=layer: (l, 0, 0, 0)
                )
                prob_spec = pl.BlockSpec((parts, q_rows, block_rows), lambda i, s, m: (0, 0, 0))
                new_spec = pl.BlockSpec((q_rows, dim), lambda i, s, m: (0, 0))
                if kind == 0:
                    pool, *weights[layer, group] = pl.pallas_call(
                        functools.partial(far_key_kernel, parts),
                        grid_spec=pltpu.PrefetchScalarGridSpec(
                            num_scalar_prefetch=2,
                            grid=(1,),
                            in_specs=piece_specs(pieces) + [row_spec, fresh_spec, hbm_spec],
                            out_specs=[pool_spec, prob_spec, new_spec],
                        ),
                        out_shape=(
                            pool_shape,
                            jax.ShapeDtypeStruct((parts, q_rows, block_rows), jnp.bfloat16),
                            jax.ShapeDtypeStruct((q_rows, dim), jnp.float32),
                        ),
                        input_output_aliases={parts + 4: 0},
                        name="far_keys",
                    )(slots, meta, *pieces, queries, fresh, pool)
                elif (kind, layer, group) != final:
                    pool, out = pl.pallas_call(
                        functools.partial(far_value_kernel, parts, heads),
                        grid_spec=pltpu.PrefetchScalarGridSpec(
                            num_scalar_prefetch=2,
                            grid=(1,),
                            in_specs=piece_specs(pieces)
                            + [prob_spec, new_spec, fresh_spec, row_spec, hbm_spec],
                            out_specs=[pool_spec, row_spec],
                        ),
                        out_shape=(pool_shape, out_shape),
                        input_output_aliases={parts + 5: 1, parts + 6: 0},
                        name="far_values",
                    )(slots, meta, *pieces, *weights[layer, group], fresh, out, pool)
    block_shape = pltpu.VMEM((1, slot_count, PAGE, dim), kv_prefill.dtype)
    kept_shapes = [
        block_shape,
        pltpu.VMEM((q_rows, dim), jnp.float32),
        pltpu.VMEM((1, dim), jnp.float32),
        pltpu.VMEM((q_rows, tail_pages * PAGE), jnp.bfloat16),
    ]
    piece_shapes = [pltpu.VMEM(piece.shape, piece.dtype) for piece in pieces + [tail]]
    *_, block, mix, token, rest = pl.pallas_call(
        functools.partial(block_kernel, parts, heads, layers - 1),
        in_specs=[smem_spec] * 2 + [vmem_spec] * (parts + 4),
        out_specs=[vmem_spec] * (parts + 4),
        out_shape=piece_shapes[:-1]
        + kept_shapes,
        input_output_aliases={2 + e: e for e in range(parts)},
        name="last_block",
    )(slots, meta, *pieces, *weights[layers - 1, heads - 1], fresh, out)
    *_, pool, out = pl.pallas_call(
        functools.partial(tail_kernel, parts, heads, layers - 1, pages),
        in_specs=[smem_spec] * 2 + [vmem_spec] * 5 + [hbm_spec] * 2,
        out_specs=[vmem_spec] * 5 + [hbm_spec] * 2,
        out_shape=(piece_shapes[-1], *kept_shapes, pool_shape, out_shape),
        scratch_shapes=[
            pltpu.VMEM((q_rows, dim), queries.dtype),
            pltpu.SemaphoreType.DMA((5,)),
        ],
        input_output_aliases={2 + i: i for i in range(7)},
        name="tail_values",
    )(slots, meta, tail, block, mix, token, rest, pool, out)
    return pool, out


def body(kv_prefill, *rest):
    ranks = lax.axis_size("seq")
    block_rows = kv_prefill.shape[3]
    parts = CTX // block_rows
    if KVH % lax.axis_size("tp") == 0 and KVH // lax.axis_size("tp") * parts == ranks:
        return streamed(kv_prefill, *rest)
    return gathered(kv_prefill, *rest)


def solution(mesh):
    placed = (
        P(None, None, "groups", ("tp", "seq"), None),
        P(None, ("groups", "seq"), "tp", None),
        P(None, None, ("groups", "seq"), None, None),
        P(("groups", "seq")),
        P(("groups", "seq"), None),
    )
    return jax.shard_map(
        body,
        mesh=mesh,
        in_specs=placed,
        out_specs=(
            P(None, None, "tp", ("groups", "seq"), None, None),
            P(None, ("groups", "seq"), "tp", None),
        ),
        check_vma=False,
    )
```

profile of v0, /device:TPU:0, one launch (start us, length us, event | category | flops | bytes accessed | tf_op | source)
XLA Modules:
  0.0 273.5 jit_solution(6259175706997655637)
XLA Ops:
  0.6 0.0 copy-start
  0.6 175.9 %cut.2 = (bf16[1,1,128,16,128]{4,3,2,1,0:T(8,128)(2,1)}, bf16[2,2,128,16,128]{4,3,2,1,0:T(8,128)(2,1)}, bf16[1,1,128,16,128]{4,3,2,1,0:T(8,128)(2,1)}, bf16[1,1,...) custom-call(bf16[2,2,4,128,16,128]{5,4,3,2,1,0:T(8,128)(2,1)} %bitca, ...), custom_call_target="tpu_custom_call" | custom-call | tf_op jit(solution)/shard_map/cut/pallas_call | solution.py:348
  176.6 0.0 copy-start.9
  176.6 0.0 copy-start.8
  176.6 0.0 copy-start.7
  176.6 0.6 collective-permute-start.7
  177.2 1.0 cut.3
  178.2 2.7 collective-permute-start.5
  180.9 0.0 copy-done.9
  180.9 0.1 collective-permute-start.3
  181.0 1.4 collective-permute-start.4
  182.3 0.0 copy-done.8
  182.3 0.4 collective-permute-start.6
  182.7 10.9 %collective-permute-done.5 = bf16[1,1,128,16,128]{4,3,2,1,0:T(8,128)(2,1)S(1)} collective-permute-done((bf16[1,1,128,16,128]{4,3,2,1,0:T(8,128)(2,1)S(1)}, bf16[1,1,128,16,128]{4,3,2,1,0:T(8,128)(2,1)S(1)}, u32[]{:S(2)}, u32[]{:S(2)}) %collective-permute-start.5) | collective-permute-done | bytes 524320 | tf_op jit(solution)/shard_map/ppermute | solution.py:384
  193.7 0.0 copy-start.4
  193.7 2.0 collective-permute-start.8
  195.7 9.2 %collective-permute-done.3 = bf16[1,1,128,16,128]{4,3,2,1,0:T(8,128)(2,1)S(1)} collective-permute-done((bf16[1,1,128,16,128]{4,3,2,1,0:T(8,128)(2,1)S(1)}, bf16[1,1,128,16,128]{4,3,2,1,0:T(8,128)(2,1)S(1)}, u32[]{:S(2)}, u32[]{:S(2)}) %collective-permute-start.3) | collective-permute-done | bytes 524320 | tf_op jit(solution)/shard_map/ppermute | solution.py:384
  204.9 0.0 copy-done.4
  204.9 0.0 copy-start.3
  204.9 0.6 collective-permute-start.9
  205.5 10.3 %collective-permute-done.4 = bf16[1,1,128,16,128]{4,3,2,1,0:T(8,128)(2,1)S(1)} collective-permute-done((bf16[1,1,128,16,128]{4,3,2,1,0:T(8,128)(2,1)}, bf16[1,1,128,16,128]{4,3,2,1,0:T(8,128)(2,1)S(1)}, u32[]{:S(2)}, u32[]{:S(2)}) %collective-permute-start.4) | collective-permute-done | bytes 524320 | tf_op jit(solution)/shard_map/ppermute | solution.py:384
  215.8 0.0 copy-start.5
  215.8 0.8 copy-done.5
  216.5 0.0 copy-done.7
  216.6 1.2 collective-permute-start.1
  217.8 9.1 %collective-permute-done.6 = bf16[1,1,128,16,128]{4,3,2,1,0:T(8,128)(2,1)S(1)} collective-permute-done((bf16[1,1,128,16,128]{4,3,2,1,0:T(8,128)(2,1)S(1)}, bf16[1,1,128,16,128]{4,3,2,1,0:T(8,128)(2,1)S(1)}, u32[]{:S(2)}, u32[]{:S(2)}) %collective-permute-start.6) | collective-permute-done | bytes 524320 | tf_op jit(solution)/shard_map/ppermute | solution.py:384
  226.9 0.8 copy-done.6
  227.7 1.9 collective-permute-start.2
  230.3 0.0 copy-done
  230.3 0.0 collective-permute-done.7.refs_0_
  230.3 0.1 collective-permute-start
  230.4 0.6 add_add_fusion.meta
  231.0 0.6 copy.22.refs_2_.refs_3_.refs_4_
  231.6 0.6 add_add_fusion.1.meta
  232.2 6.1 %own_head.1 = (bf16[2,2,2,256,16,128]{5,4,3,2,1,0:T(8,128)(2,1)}, bf16[2,1,16,128]{3,2,1,0:T(8,128)(2,1)}) custom-call(s32[256]{0:T(256)} %bitcast.29, s32[4]{0:T(128)} %add_add_fusion.1.meta, bf16[2,2,4,128,16,128]{5,4,3,2,1,0:T(8,128)(2,1)} %bitcast.22, bf16[2,2,128,16,128]{4,3,2,1,0:T(8,128)(2,1)} %collective-permute-done.7.refs_0_, ...), custom_call_target="tpu_custom_call" | custom-call | tf_op jit(solution)/shard_map/own_head/pallas_call | solution.py:396
  238.4 3.8 %far_keys.2 = (bf16[2,2,2,256,16,128]{5,4,3,2,1,0:T(8,128)(2,1)}, bf16[2,16,2048]{2,1,0:T(8,128)(2,1)}, f32[16,128]{1,0:T(8,128)}) custom-call(s32[256]{0:T(256)} %bitcast.30, s32[4]{0:T(128)} %add_add_fusion.meta, bf16[1,128,16,128]{3,2,1,0:T(8,128)(2,1)} %bitcast.26, bf16[1,128,16,128]{3,2,1,0:T(8,128)(2,1)} %bitcast.28, ...), custom_call_target="tpu_custom_call", output_to_operand_aliasing={{0}: (6, {})} | custom-call | tf_op jit(solution)/shard_map/far_keys/pallas_call | solution.py:445
  242.2 0.0 copy-done.3
  242.2 3.8 %far_keys.3 = (bf16[2,2,2,256,16,128]{5,4,3,2,1,0:T(8,128)(2,1)}, bf16[2,16,2048]{2,1,0:T(8,128)(2,1)}, f32[16,128]{1,0:T(8,128)}) custom-call(s32[256]{0:T(256)} %bitcast.31, s32[4]{0:T(128)} %add_add_fusion.meta, bf16[1,128,16,128]{3,2,1,0:T(8,128)(2,1)} %bitcast.25, bf16[1,128,16,128]{3,2,1,0:T(8,128)(2,1)} %bitcast.27, ...), custom_call_target="tpu_custom_call", output_to_operand_aliasing={{0}: (6, {})} | custom-call | tf_op jit(solution)/shard_map/far_keys/pallas_call | solution.py:445
  246.0 0.0 collective-permute-done.8
  246.0 3.5 %collective-permute-done.9 = bf16[1,1,128,16,128]{4,3,2,1,0:T(8,128)(2,1)S(1)} collective-permute-done((bf16[1,1,128,16,128]{4,3,2,1,0:T(8,128)(2,1)}, bf16[1,1,128,16,128]{4,3,2,1,0:T(8,128)(2,1)S(1)}, u32[]{:S(2)}, u32[]{:S(2)}) %collective-permute-start.9) | collective-permute-done | bytes 524320 | tf_op jit(solution)/shard_map/ppermute | solution.py:384
  249.5 0.0 copy-done.1
  249.5 0.8 copy-done.2
  250.3 3.4 %far_values.1 = (bf16[2,2,2,256,16,128]{5,4,3,2,1,0:T(8,128)(2,1)}, bf16[2,1,16,128]{3,2,1,0:T(8,128)(2,1)}) custom-call(s32[256]{0:T(256)} %bitcast.32, s32[4]{0:T(128)} %add_add_fusion.meta, bf16[1,128,16,128]{3,2,1,0:T(8,128)(2,1)} %bitcast.23, bf16[1,128,16,128]{3,2,1,0:T(8,128)(2,1)} %bitcast.24, ...), custom_call_target="tpu_custom_call", output_to_operand_aliasing={{1}: (7, {}), {0}: (8, {})} | custom-call | tf_op jit(solution)/shard_map/far_values/pallas_call | solution.py:462
  253.7 15.4 %collective-permute-done.2 = bf16[1,1,96,16,128]{4,3,2,1,0:T(8,128)(2,1)S(1)} collective-permute-done((bf16[1,1,96,16,128]{4,3,2,1,0:T(8,128)(2,1)}, bf16[1,1,96,16,128]{4,3,2,1,0:T(8,128)(2,1)S(1)}, u32[]{:S(2)}, u32[]{:S(2)}) %collective-permute-start.2) | collective-permute-done | bytes 393248 | tf_op jit(solution)/shard_map/ppermute | solution.py:384
  269.1 0.0 collective-permute-done.1
  269.1 1.5 last_block.1
  270.7 1.0 collective-permute-done
  271.7 1.8 tail_values.1
  (4 shorter events, 0.0 us)
Async XLA Ops:
  0.6 229.6 %copy-start = (bf16[2,2,1,8,128]{4,3,2,1,0:T(8,128)(2,1)S(1)}, bf16[2,2,1,8,128]{4,3,2,1,0:T(8,128)(2,1)}, u32[]{:S(2)}) copy-start(bf16[2,2,1,8,128]{4,3,2,1,0:T(8,128)(2,1)} %param.7) | copy-start | bytes 24580
  176.6 4.3 %copy-start.9 = (bf16[1,1,128,16,128]{4,3,2,1,0:T(8,128)(2,1)S(1)}, bf16[1,1,128,16,128]{4,3,2,1,0:T(8,128)(2,1)}, u32[]{:S(2)}) copy-start(bf16[1,1,128,16,128]{4,3,2,1,0:T(8,128)(2,1)} %get-tuple-element.30) | copy-start | bytes 1572868
  176.6 5.8 %copy-start.8 = (bf16[1,1,128,16,128]{4,3,2,1,0:T(8,128)(2,1)S(1)}, bf16[1,1,128,16,128]{4,3,2,1,0:T(8,128)(2,1)}, u32[]{:S(2)}) copy-start(bf16[1,1,128,16,128]{4,3,2,1,0:T(8,128)(2,1)} %get-tuple-element.32) | copy-start | bytes 1572868
  176.6 40.0 %copy-start.7 = (bf16[1,1,128,16,128]{4,3,2,1,0:T(8,128)(2,1)S(1)}, bf16[1,1,128,16,128]{4,3,2,1,0:T(8,128)(2,1)}, u32[]{:S(2)}) copy-start(bf16[1,1,128,16,128]{4,3,2,1,0:T(8,128)(2,1)} %get-tuple-element.28) | copy-start | bytes 1572868
  176.6 53.7 %collective-permute-start.7 = (bf16[2,2,128,16,128]{4,3,2,1,0:T(8,128)(2,1)}, bf16[2,2,128,16,128]{4,3,2,1,0:T(8,128)(2,1)}, u32[]{:S(2)}, u32[]{:S(2)}) collective-permute-start(bf16[2,2,128,16,128]{4,3,2,1,0:T(8,128)(2,1)} %get-tuple-element.33), channel_id=1, source_target_pairs={{0,1},{1,0},{2,3},{3,2},{4,5},{5,4},{6,7},{7,6},{8,9},{9,8},{10,11... | collective-permute-start | bytes 6291464 | tf_op jit(solution)/shard_map/ppermute | solution.py:384
  178.2 15.4 %collective-permute-start.5 = (bf16[1,1,128,16,128]{4,3,2,1,0:T(8,128)(2,1)S(1)}, bf16[1,1,128,16,128]{4,3,2,1,0:T(8,128)(2,1)S(1)}, u32[]{:S(2)}, u32[]{:S(2)}) collective-permute-start(bf16[1,1,128,16,128]{4,3,2,1,0:T(8,128)(2,1)S(1)} %cut.3), channel_id=1, source_target_pairs={{0,2},{1,3},{2,0},{3,1},{4,6},{5,7},{6,4},{7,5},{8,10},{9,11},{10,... | collective-permute-start | bytes 1572872 | tf_op jit(solution)/shard_map/ppermute | solution.py:384
  180.9 24.0 %collective-permute-start.3 = (bf16[1,1,128,16,128]{4,3,2,1,0:T(8,128)(2,1)S(1)}, bf16[1,1,128,16,128]{4,3,2,1,0:T(8,128)(2,1)S(1)}, u32[]{:S(2)}, u32[]{:S(2)}) collective-permute-start(bf16[1,1,128,16,128]{4,3,2,1,0:T(8,128)(2,1)S(1)} %copy-done.9), channel_id=1, source_target_pairs={{0,2},{1,3},{2,0},{3,1},{4,6},{5,7},{6,4},{7,5},{8,10},{9,11},{10,... | collective-permute-start | bytes 1572872 | tf_op jit(solution)/shard_map/ppermute | solution.py:384
  181.0 34.8 %collective-permute-start.4 = (bf16[1,1,128,16,128]{4,3,2,1,0:T(8,128)(2,1)}, bf16[1,1,128,16,128]{4,3,2,1,0:T(8,128)(2,1)S(1)}, u32[]{:S(2)}, u32[]{:S(2)}) collective-permute-start(bf16[1,1,128,16,128]{4,3,2,1,0:T(8,128)(2,1)} %get-tuple-element.31), channel_id=1, source_target_pairs={{0,3},{1,2},{2,1},{3,0},{4,7},{5,6},{6,5},{7,4},{8,11},{9,10},{10,... | collective-permute-start | bytes 1572872 | tf_op jit(solution)/shard_map/ppermute | solution.py:384
  182.3 44.6 %collective-permute-start.6 = (bf16[1,1,128,16,128]{4,3,2,1,0:T(8,128)(2,1)S(1)}, bf16[1,1,128,16,128]{4,3,2,1,0:T(8,128)(2,1)S(1)}, u32[]{:S(2)}, u32[]{:S(2)}) collective-permute-start(bf16[1,1,128,16,128]{4,3,2,1,0:T(8,128)(2,1)S(1)} %copy-done.8), channel_id=1, source_target_pairs={{0,3},{1,2},{2,1},{3,0},{4,7},{5,6},{6,5},{7,4},{8,11},{9,10},{10,... | collective-permute-start | bytes 1572872 | tf_op jit(solution)/shard_map/ppermute | solution.py:384
  193.7 11.2 %copy-start.4 = (bf16[1,1,128,16,128]{4,3,2,1,0:T(8,128)(2,1)}, bf16[1,1,128,16,128]{4,3,2,1,0:T(8,128)(2,1)S(1)}, u32[]{:S(2)}) copy-start(bf16[1,1,128,16,128]{4,3,2,1,0:T(8,128)(2,1)S(1)} %collective-permute-done.5) | copy-start | bytes 1572868
  193.7 52.3 %collective-permute-start.8 = (bf16[1,1,128,16,128]{4,3,2,1,0:T(8,128)(2,1)}, bf16[1,1,128,16,128]{4,3,2,1,0:T(8,128)(2,1)S(1)}, u32[]{:S(2)}, u32[]{:S(2)}) collective-permute-start(bf16[1,1,128,16,128]{4,3,2,1,0:T(8,128)(2,1)} %get-tuple-element.38), channel_id=1, source_target_pairs={{0,2},{1,3},{2,0},{3,1},{4,6},{5,7},{6,4},{7,5},{8,10},{9,11},{10,... | collective-permute-start | bytes 1572872 | tf_op jit(solution)/shard_map/ppermute | solution.py:384
  204.9 37.3 %copy-start.3 = (bf16[1,1,128,16,128]{4,3,2,1,0:T(8,128)(2,1)}, bf16[1,1,128,16,128]{4,3,2,1,0:T(8,128)(2,1)S(1)}, u32[]{:S(2)}) copy-start(bf16[1,1,128,16,128]{4,3,2,1,0:T(8,128)(2,1)S(1)} %collective-permute-done.3) | copy-start | bytes 1572868
  204.9 44.6 %collective-permute-start.9 = (bf16[1,1,128,16,128]{4,3,2,1,0:T(8,128)(2,1)}, bf16[1,1,128,16,128]{4,3,2,1,0:T(8,128)(2,1)S(1)}, u32[]{:S(2)}, u32[]{:S(2)}) collective-permute-start(bf16[1,1,128,16,128]{4,3,2,1,0:T(8,128)(2,1)} %get-tuple-element.39), channel_id=1, source_target_pairs={{0,3},{1,2},{2,1},{3,0},{4,7},{5,6},{6,5},{7,4},{8,11},{9,10},{10,... | collective-permute-start | bytes 1572872 | tf_op jit(solution)/shard_map/ppermute | solution.py:384
  215.8 0.8 copy-start.5
  216.6 52.6 %collective-permute-start.1 = (bf16[1,1,128,16,128]{4,3,2,1,0:T(8,128)(2,1)S(1)}, bf16[1,1,128,16,128]{4,3,2,1,0:T(8,128)(2,1)S(1)}, u32[]{:S(2)}, u32[]{:S(2)}) collective-permute-start(bf16[1,1,128,16,128]{4,3,2,1,0:T(8,128)(2,1)S(1)} %copy-done.7), channel_id=1, source_target_pairs={{0,2},{1,3},{2,0},{3,1},{4,6},{5,7},{6,4},{7,5},{8,10},{9,11},{10,... | collective-permute-start | bytes 1572872 | tf_op jit(solution)/shard_map/ppermute | solution.py:384
  226.9 0.8 copy-start.6
  227.7 41.4 %collective-permute-start.2 = (bf16[1,1,96,16,128]{4,3,2,1,0:T(8,128)(2,1)}, bf16[1,1,96,16,128]{4,3,2,1,0:T(8,128)(2,1)S(1)}, u32[]{:S(2)}, u32[]{:S(2)}) collective-permute-start(bf16[1,1,96,16,128]{4,3,2,1,0:T(8,128)(2,1)} %get-tuple-element.29), channel_id=1, source_target_pairs={{0,3},{1,2},{2,1},{3,0},{4,7},{5,6},{6,5},{7,4},{8,11},{9,10},{10,... | collective-permute-start | bytes 1179656 | tf_op jit(solution)/shard_map/ppermute | solution.py:384
  230.3 41.4 %collective-permute-start = (bf16[1,1,32,16,128]{4,3,2,1,0:T(8,128)(2,1)}, bf16[1,1,32,16,128]{4,3,2,1,0:T(8,128)(2,1)S(1)}, u32[]{:S(2)}, u32[]{:S(2)}) collective-permute-start(bf16[1,1,32,16,128]{4,3,2,1,0:T(8,128)(2,1)} %get-tuple-element.27), channel_id=1, source_target_pairs={{0,3},{1,2},{2,1},{3,0},{4,7},{5,6},{6,5},{7,4},{8,11},{9,10},{10,... | collective-permute-start | bytes 393224 | tf_op jit(solution)/shard_map/ppermute | solution.py:384
  246.0 3.5 %copy-start.1 = (bf16[1,1,128,16,128]{4,3,2,1,0:T(8,128)(2,1)}, bf16[1,1,128,16,128]{4,3,2,1,0:T(8,128)(2,1)S(1)}, u32[]{:S(2)}) copy-start(bf16[1,1,128,16,128]{4,3,2,1,0:T(8,128)(2,1)S(1)} %collective-permute-done.8) | copy-start | bytes 1572868
  249.5 0.8 copy-start.2
where the time goes:
time: 274 us; the launch traced here: 273 us
  Pallas kernels  197 us (72%)
  waiting for transfers between devices  59.5 us (22%)
  starting transfers between devices  10.8 us (4%)
  local copies, waits for them, and re-layouts  3.01 us (1%)
    pallas_call x2, Pallas kernels, cut(): pl.pallas_call(functools.partial(cut_kernel, [entry[:4] for entry in want...  177 us
    ppermute x10, waiting for transfers between devices, streamed(): received[key] = lax.ppermute(cuts[i], 'seq', pairs)  59.5 us
    ppermute x10, starting transfers between devices, streamed(): received[key] = lax.ppermute(cuts[i], 'seq', pairs)  10.8 us
    pallas_call x2, Pallas kernels, streamed(): pl.pallas_call(functools.partial(far_key_kernel, parts), grid_spec=pltpu....  7.61 us
    pallas_call x1, Pallas kernels, streamed(): pl.pallas_call(functools.partial(own_kernel, parts, heads), grid_spec=plt...  6.13 us
  transfers between devices with their start and end apart: 10, of which 7 were waited for; matrix products, arithmetic and copies ran while one was open for 1% of the time, Pallas kernels for 7%

commit v1 on v0

--- a/solution.py
+++ b/solution.py
@@ -301,25 +301,37 @@
         store.wait()
 
 
-def cut_kernel(starts, src, *refs):
-    outs, sems = refs[:-1], refs[-1]
+def cut_kernel(starts, bounced, src, *refs):
+    outs, refs = refs[: len(starts)], refs[len(starts) :]
+    load_sems, store_sems = refs[-2:]
+    held = refs[:-2] if bounced else outs
     me = lax.axis_index("seq")
-    copies = []
+    loads, stores = [], []
     for i, (distance, kind, layer, page) in enumerate(starts):
         kinds, layers, pages = outs[i].shape[0], outs[i].shape[1], outs[i].shape[2]
         for k in range(kinds):
             for l in range(layers):
-                copies.append(
+                loads.append(
                     pltpu.make_async_copy(
                         src.at[kind + k, layer + l, me ^ distance, pl.ds(page, pages)],
-                        outs[i].at[k, l],
-                        sems.at[len(copies)],
+                        held[i].at[k, l],
+                        load_sems.at[len(loads)],
                     )
                 )
-    for copy in copies:
-        copy.start()
-    for copy in copies:
-        copy.wait()
+                if bounced:
+                    stores.append(
+                        pltpu.make_async_copy(
+                            held[i].at[k, l], outs[i].at[k, l], store_sems.at[len(stores)]
+                        )
+                    )
+    for load in loads:
+        load.start()
+    for i, load in enumerate(loads):
+        load.wait()
+        if bounced:
+            stores[i].start()
+    for store in stores:
+        store.wait()
 
 
 def streamed(kv_prefill, queries, new_kv, lengths, page_slots):
@@ -346,7 +358,7 @@
     def cut(wanted, near_core):
         shapes = [entry[4:] + (PAGE, dim) for entry in wanted]
         return pl.pallas_call(
-            functools.partial(cut_kernel, [entry[:4] for entry in wanted]),
+            functools.partial(cut_kernel, [entry[:4] for entry in wanted], not near_core),
             in_specs=[hbm_spec],
             out_specs=[vmem_spec if near_core else hbm_spec] * len(wanted),
             out_shape=[
@@ -355,7 +367,8 @@
                 else jax.ShapeDtypeStruct(shape, kv_prefill.dtype)
                 for shape in shapes
             ],
-            scratch_shapes=[pltpu.SemaphoreType.DMA((sum(s[0] * s[1] for s in shapes),))],
+            scratch_shapes=([] if near_core else [pltpu.VMEM(s, kv_prefill.dtype) for s in shapes])
+            + [pltpu.SemaphoreType.DMA((sum(s[0] * s[1] for s in shapes),))] * 2,
             name="cut",
         )(paged)
 

time: 274 us -> 103 us (0.38)
  Pallas kernels: 197 us -> 26.6 us
    pallas_call x2, Pallas kernels: 177 us -> 6.16 us  [cut(): pl.pallas_call(functools.partial(cut_kernel, [entry[:4] for entry in want...]
  transfers between devices with their start and end apart: 10 -> 10, of which waited for: 7 -> 7; matrix products, arithmetic and copies ran while one was open for 1% -> 2% of each run, Pallas kernels for 7% -> 19%
where the time goes in v1:
time: 103 us
  waiting for transfers between devices  59.5 us (58%)
  Pallas kernels  26.6 us (26%)
  starting transfers between devices  10.8 us (10%)
  local copies, waits for them, and re-layouts  3.01 us (3%)
  between operations  1.39 us (1%)
  other arithmetic  1.27 us (1%)
    ppermute x10, waiting for transfers between devices, streamed(): received[key] = lax.ppermute(cuts[i], 'seq', pairs)  59.5 us
    ppermute x10, starting transfers between devices, streamed(): received[key] = lax.ppermute(cuts[i], 'seq', pairs)  10.8 us
    pallas_call x2, Pallas kernels, streamed(): pl.pallas_call(functools.partial(far_key_kernel, parts), grid_spec=pltpu....  7.61 us
    pallas_call x2, Pallas kernels, cut(): pl.pallas_call(functools.partial(cut_kernel, [entry[:4] for entry in want...  6.16 us
    pallas_call x1, Pallas kernels, streamed(): pl.pallas_call(functools.partial(own_kernel, parts, heads), grid_spec=plt...  6.13 us
    pallas_call x1, Pallas kernels, streamed(): pl.pallas_call(functools.partial(far_value_kernel, parts, heads), grid_sp...  3.45 us
    unnamed x20, local copies, waits for them, and re-layouts  2.41 us
  transfers between devices with their start and end apart: 10, of which 7 were waited for; matrix products, arithmetic and copies ran while one was open for 2% of the time, Pallas kernels for 19%

profile of v1, /device:TPU:0, one launch (start us, length us, event | category | flops | bytes accessed | tf_op | source)
XLA Modules:
  0.0 102.7 jit_solution(12217073692481416644)
XLA Ops:
  0.6 0.0 copy-start
  0.6 5.1 %cut.2 = (bf16[1,1,128,16,128]{4,3,2,1,0:T(8,128)(2,1)}, bf16[2,2,128,16,128]{4,3,2,1,0:T(8,128)(2,1)}, bf16[1,1,128,16,128]{4,3,2,1,0:T(8,128)(2,1)}, bf16[1,1,...) custom-call(bf16[2,2,4,128,16,128]{5,4,3,2,1,0:T(8,128)(2,1)} %bitca, ...), custom_call_target="tpu_custom_call" | custom-call | tf_op jit(solution)/shard_map/cut/pallas_call | solution.py:360
  5.8 0.0 copy-start.9
  5.8 0.0 copy-start.8
  5.8 0.0 copy-start.7
  5.8 0.6 collective-permute-start.7
  6.3 1.1 %cut.3 = bf16[1,1,128,16,128]{4,3,2,1,0:T(8,128)(2,1)S(1)} custom-call(bf16[2,2,4,128,16,128]{5,4,3,2,1,0:T(8,128)(2,1)} %bitcast.21), custom_call_target="tpu_custom_call" | custom-call | tf_op jit(solution)/shard_map/cut/pallas_call | solution.py:360
  7.4 2.7 %collective-permute-start.5 = (bf16[1,1,128,16,128]{4,3,2,1,0:T(8,128)(2,1)S(1)}, bf16[1,1,128,16,128]{4,3,2,1,0:T(8,128)(2,1)S(1)}, u32[]{:S(2)}, u32[]{:S(2)}) collective-permute-start(bf16[1,1,128,16,128]{4,3,2,1,0:T(8,128)(2,1)S(1)} %cut.3), channel_id=1, source_target_pairs={{0,2},{1,3},{2,0},{3,1},{4,6},{5,7},{6,4},{7,5},{8,10},{9,11},{10,... | collective-permute-start | bytes 1572872 | tf_op jit(solution)/shard_map/ppermute | solution.py:397
  10.1 0.0 copy-done.9
  10.1 0.1 collective-permute-start.3
  10.2 1.4 %collective-permute-start.4 = (bf16[1,1,128,16,128]{4,3,2,1,0:T(8,128)(2,1)}, bf16[1,1,128,16,128]{4,3,2,1,0:T(8,128)(2,1)S(1)}, u32[]{:S(2)}, u32[]{:S(2)}) collective-permute-start(bf16[1,1,128,16,128]{4,3,2,1,0:T(8,128)(2,1)} %get-tuple-element.31), channel_id=1, source_target_pairs={{0,3},{1,2},{2,1},{3,0},{4,7},{5,6},{6,5},{7,4},{8,11},{9,10},{10,... | collective-permute-start | bytes 1572872 | tf_op jit(solution)/shard_map/ppermute | solution.py:397
  11.5 0.0 copy-done.8
  11.5 0.4 collective-permute-start.6
  11.9 10.9 %collective-permute-done.5 = bf16[1,1,128,16,128]{4,3,2,1,0:T(8,128)(2,1)S(1)} collective-permute-done((bf16[1,1,128,16,128]{4,3,2,1,0:T(8,128)(2,1)S(1)}, bf16[1,1,128,16,128]{4,3,2,1,0:T(8,128)(2,1)S(1)}, u32[]{:S(2)}, u32[]{:S(2)}) %collective-permute-start.5) | collective-permute-done | bytes 524320 | tf_op jit(solution)/shard_map/ppermute | solution.py:397
  22.8 0.0 copy-start.4
  22.8 2.0 %collective-permute-start.8 = (bf16[1,1,128,16,128]{4,3,2,1,0:T(8,128)(2,1)}, bf16[1,1,128,16,128]{4,3,2,1,0:T(8,128)(2,1)S(1)}, u32[]{:S(2)}, u32[]{:S(2)}) collective-permute-start(bf16[1,1,128,16,128]{4,3,2,1,0:T(8,128)(2,1)} %get-tuple-element.38), channel_id=1, source_target_pairs={{0,2},{1,3},{2,0},{3,1},{4,6},{5,7},{6,4},{7,5},{8,10},{9,11},{10,... | collective-permute-start | bytes 1572872 | tf_op jit(solution)/shard_map/ppermute | solution.py:397
  24.9 9.2 %collective-permute-done.3 = bf16[1,1,128,16,128]{4,3,2,1,0:T(8,128)(2,1)S(1)} collective-permute-done((bf16[1,1,128,16,128]{4,3,2,1,0:T(8,128)(2,1)S(1)}, bf16[1,1,128,16,128]{4,3,2,1,0:T(8,128)(2,1)S(1)}, u32[]{:S(2)}, u32[]{:S(2)}) %collective-permute-start.3) | collective-permute-done | bytes 524320 | tf_op jit(solution)/shard_map/ppermute | solution.py:397
  34.1 0.0 copy-done.4
  34.1 0.0 copy-start.3
  34.1 0.6 collective-permute-start.9
  34.7 10.3 %collective-permute-done.4 = bf16[1,1,128,16,128]{4,3,2,1,0:T(8,128)(2,1)S(1)} collective-permute-done((bf16[1,1,128,16,128]{4,3,2,1,0:T(8,128)(2,1)}, bf16[1,1,128,16,128]{4,3,2,1,0:T(8,128)(2,1)S(1)}, u32[]{:S(2)}, u32[]{:S(2)}) %collective-permute-start.4) | collective-permute-done | bytes 524320 | tf_op jit(solution)/shard_map/ppermute | solution.py:397
  45.0 0.0 copy-start.5
  45.0 0.8 copy-done.5
  45.7 0.0 copy-done.7
  45.7 1.2 %collective-permute-start.1 = (bf16[1,1,128,16,128]{4,3,2,1,0:T(8,128)(2,1)S(1)}, bf16[1,1,128,16,128]{4,3,2,1,0:T(8,128)(2,1)S(1)}, u32[]{:S(2)}, u32[]{:S(2)}) collective-permute-start(bf16[1,1,128,16,128]{4,3,2,1,0:T(8,128)(2,1)S(1)} %copy-done.7), channel_id=1, source_target_pairs={{0,2},{1,3},{2,0},{3,1},{4,6},{5,7},{6,4},{7,5},{8,10},{9,11},{10,... | collective-permute-start | bytes 1572872 | tf_op jit(solution)/shard_map/ppermute | solution.py:397
  47.0 9.1 %collective-permute-done.6 = bf16[1,1,128,16,128]{4,3,2,1,0:T(8,128)(2,1)S(1)} collective-permute-done((bf16[1,1,128,16,128]{4,3,2,1,0:T(8,128)(2,1)S(1)}, bf16[1,1,128,16,128]{4,3,2,1,0:T(8,128)(2,1)S(1)}, u32[]{:S(2)}, u32[]{:S(2)}) %collective-permute-start.6) | collective-permute-done | bytes 524320 | tf_op jit(solution)/shard_map/ppermute | solution.py:397
  56.1 0.8 copy-done.6
  56.9 1.9 %collective-permute-start.2 = (bf16[1,1,96,16,128]{4,3,2,1,0:T(8,128)(2,1)}, bf16[1,1,96,16,128]{4,3,2,1,0:T(8,128)(2,1)S(1)}, u32[]{:S(2)}, u32[]{:S(2)}) collective-permute-start(bf16[1,1,96,16,128]{4,3,2,1,0:T(8,128)(2,1)} %get-tuple-element.29), channel_id=1, source_target_pairs={{0,3},{1,2},{2,1},{3,0},{4,7},{5,6},{6,5},{7,4},{8,11},{9,10},{10,... | collective-permute-start | bytes 1179656 | tf_op jit(solution)/shard_map/ppermute | solution.py:397
  59.5 0.0 copy-done
  59.5 0.0 collective-permute-done.7.refs_0_
  59.5 0.1 collective-permute-start
  59.6 0.6 add_add_fusion.meta
  60.2 0.6 copy.22.refs_2_.refs_3_.refs_4_
  60.8 0.6 add_add_fusion.1.meta
  61.4 6.1 %own_head.1 = (bf16[2,2,2,256,16,128]{5,4,3,2,1,0:T(8,128)(2,1)}, bf16[2,1,16,128]{3,2,1,0:T(8,128)(2,1)}) custom-call(s32[256]{0:T(256)} %bitcast.29, s32[4]{0:T(128)} %add_add_fusion.1.meta, bf16[2,2,4,128,16,128]{5,4,3,2,1,0:T(8,128)(2,1)} %bitcast.22, bf16[2,2,128,16,128]{4,3,2,1,0:T(8,128)(2,1)} %collective-permute-done.7.refs_0_, ...), custom_call_target="tpu_custom_call" | custom-call | tf_op jit(solution)/shard_map/own_head/pallas_call | solution.py:409
  67.6 3.8 %far_keys.2 = (bf16[2,2,2,256,16,128]{5,4,3,2,1,0:T(8,128)(2,1)}, bf16[2,16,2048]{2,1,0:T(8,128)(2,1)}, f32[16,128]{1,0:T(8,128)}) custom-call(s32[256]{0:T(256)} %bitcast.30, s32[4]{0:T(128)} %add_add_fusion.meta, bf16[1,128,16,128]{3,2,1,0:T(8,128)(2,1)} %bitcast.26, bf16[1,128,16,128]{3,2,1,0:T(8,128)(2,1)} %bitcast.28, ...), custom_call_target="tpu_custom_call", output_to_operand_aliasing={{0}: (6, {})} | custom-call | tf_op jit(solution)/shard_map/far_keys/pallas_call | solution.py:458
  71.4 0.0 copy-done.3
  71.4 3.8 %far_keys.3 = (bf16[2,2,2,256,16,128]{5,4,3,2,1,0:T(8,128)(2,1)}, bf16[2,16,2048]{2,1,0:T(8,128)(2,1)}, f32[16,128]{1,0:T(8,128)}) custom-call(s32[256]{0:T(256)} %bitcast.31, s32[4]{0:T(128)} %add_add_fusion.meta, bf16[1,128,16,128]{3,2,1,0:T(8,128)(2,1)} %bitcast.25, bf16[1,128,16,128]{3,2,1,0:T(8,128)(2,1)} %bitcast.27, ...), custom_call_target="tpu_custom_call", output_to_operand_aliasing={{0}: (6, {})} | custom-call | tf_op jit(solution)/shard_map/far_keys/pallas_call | solution.py:458
  75.2 0.0 collective-permute-done.8
  75.2 3.5 %collective-permute-done.9 = bf16[1,1,128,16,128]{4,3,2,1,0:T(8,128)(2,1)S(1)} collective-permute-done((bf16[1,1,128,16,128]{4,3,2,1,0:T(8,128)(2,1)}, bf16[1,1,128,16,128]{4,3,2,1,0:T(8,128)(2,1)S(1)}, u32[]{:S(2)}, u32[]{:S(2)}) %collective-permute-start.9) | collective-permute-done | bytes 524320 | tf_op jit(solution)/shard_map/ppermute | solution.py:397
  78.7 0.0 copy-done.1
  78.7 0.8 copy-done.2
  79.5 3.4 %far_values.1 = (bf16[2,2,2,256,16,128]{5,4,3,2,1,0:T(8,128)(2,1)}, bf16[2,1,16,128]{3,2,1,0:T(8,128)(2,1)}) custom-call(s32[256]{0:T(256)} %bitcast.32, s32[4]{0:T(128)} %add_add_fusion.meta, bf16[1,128,16,128]{3,2,1,0:T(8,128)(2,1)} %bitcast.23, bf16[1,128,16,128]{3,2,1,0:T(8,128)(2,1)} %bitcast.24, ...), custom_call_target="tpu_custom_call", output_to_operand_aliasing={{1}: (7, {}), {0}: (8, {})} | custom-call | tf_op jit(solution)/shard_map/far_values/pallas_call | solution.py:475
  82.9 15.4 %collective-permute-done.2 = bf16[1,1,96,16,128]{4,3,2,1,0:T(8,128)(2,1)S(1)} collective-permute-done((bf16[1,1,96,16,128]{4,3,2,1,0:T(8,128)(2,1)}, bf16[1,1,96,16,128]{4,3,2,1,0:T(8,128)(2,1)S(1)}, u32[]{:S(2)}, u32[]{:S(2)}) %collective-permute-start.2) | collective-permute-done | bytes 393248 | tf_op jit(solution)/shard_map/ppermute | solution.py:397
  98.3 0.0 collective-permute-done.1
  98.3 1.5 %last_block.1 = (bf16[1,128,16,128]{3,2,1,0:T(8,128)(2,1)S(1)}, bf16[1,96,16,128]{3,2,1,0:T(8,128)(2,1)S(1)}, bf16[1,256,16,128]{3,2,1,0:T(8,128)(2,1)S(1)}, f32...) custom-call(s32[256]{0:T(256)} %bitcast.33, ...), custom_call_target="tpu_custom_call", output_to_operand_aliasing={{0}: (2, {}), {1}: (3, {})} | custom-call | tf_op jit(solution)/shard_map/last_block/pallas_call | solution.py:496
  99.9 1.0 %collective-permute-done = bf16[1,1,32,16,128]{4,3,2,1,0:T(8,128)(2,1)S(1)} collective-permute-done((bf16[1,1,32,16,128]{4,3,2,1,0:T(8,128)(2,1)}, bf16[1,1,32,16,128]{4,3,2,1,0:T(8,128)(2,1)S(1)}, u32[]{:S(2)}, u32[]{:S(2)}) %collective-permute-start) | collective-permute-done | bytes 131104 | tf_op jit(solution)/shard_map/ppermute | solution.py:397
  100.9 1.8 %tail_values.1 = (bf16[1,32,16,128]{3,2,1,0:T(8,128)(2,1)S(1)}, bf16[1,256,16,128]{3,2,1,0:T(8,128)(2,1)S(1)}, f32[16,128]{1,0:T(8,128)S(1)}, f32[1,128]{1,0:T(1...) custom-call(s32[256]{0:T(256)} %bitcast.34, ...), custom_call_target="tpu_custom_call", output_to_operand_aliasing={{0}: (2, {}), {1}: (3, {}), {2}: (4, {}), {3}: (5, {}), {4}... | custom-call | tf_op jit(solution)/shard_map/tail_values/pallas_call | solution.py:505
  (4 shorter events, 0.0 us)
Async XLA Ops:
  0.6 58.8 %copy-start = (bf16[2,2,1,8,128]{4,3,2,1,0:T(8,128)(2,1)S(1)}, bf16[2,2,1,8,128]{4,3,2,1,0:T(8,128)(2,1)}, u32[]{:S(2)}) copy-start(bf16[2,2,1,8,128]{4,3,2,1,0:T(8,128)(2,1)} %param.7) | copy-start | bytes 24580
  5.8 4.3 %copy-start.9 = (bf16[1,1,128,16,128]{4,3,2,1,0:T(8,128)(2,1)S(1)}, bf16[1,1,128,16,128]{4,3,2,1,0:T(8,128)(2,1)}, u32[]{:S(2)}) copy-start(bf16[1,1,128,16,128]{4,3,2,1,0:T(8,128)(2,1)} %get-tuple-element.30) | copy-start | bytes 1572868
  5.8 5.8 %copy-start.8 = (bf16[1,1,128,16,128]{4,3,2,1,0:T(8,128)(2,1)S(1)}, bf16[1,1,128,16,128]{4,3,2,1,0:T(8,128)(2,1)}, u32[]{:S(2)}) copy-start(bf16[1,1,128,16,128]{4,3,2,1,0:T(8,128)(2,1)} %get-tuple-element.32) | copy-start | bytes 1572868
  5.8 40.0 %copy-start.7 = (bf16[1,1,128,16,128]{4,3,2,1,0:T(8,128)(2,1)S(1)}, bf16[1,1,128,16,128]{4,3,2,1,0:T(8,128)(2,1)}, u32[]{:S(2)}) copy-start(bf16[1,1,128,16,128]{4,3,2,1,0:T(8,128)(2,1)} %get-tuple-element.28) | copy-start | bytes 1572868
  5.8 53.7 %collective-permute-start.7 = (bf16[2,2,128,16,128]{4,3,2,1,0:T(8,128)(2,1)}, bf16[2,2,128,16,128]{4,3,2,1,0:T(8,128)(2,1)}, u32[]{:S(2)}, u32[]{:S(2)}) collective-permute-start(bf16[2,2,128,16,128]{4,3,2,1,0:T(8,128)(2,1)} %get-tuple-element.33), channel_id=1, source_target_pairs={{0,1},{1,0},{2,3},{3,2},{4,5},{5,4},{6,7},{7,6},{8,9},{9,8},{10,11... | collective-permute-start | bytes 6291464 | tf_op jit(solution)/shard_map/ppermute | solution.py:397
  7.4 15.4 %collective-permute-start.5 = (bf16[1,1,128,16,128]{4,3,2,1,0:T(8,128)(2,1)S(1)}, bf16[1,1,128,16,128]{4,3,2,1,0:T(8,128)(2,1)S(1)}, u32[]{:S(2)}, u32[]{:S(2)}) collective-permute-start(bf16[1,1,128,16,128]{4,3,2,1,0:T(8,128)(2,1)S(1)} %cut.3), channel_id=1, source_target_pairs={{0,2},{1,3},{2,0},{3,1},{4,6},{5,7},{6,4},{7,5},{8,10},{9,11},{10,... | collective-permute-start | bytes 1572872 | tf_op jit(solution)/shard_map/ppermute | solution.py:397
  10.1 24.0 %collective-permute-start.3 = (bf16[1,1,128,16,128]{4,3,2,1,0:T(8,128)(2,1)S(1)}, bf16[1,1,128,16,128]{4,3,2,1,0:T(8,128)(2,1)S(1)}, u32[]{:S(2)}, u32[]{:S(2)}) collective-permute-start(bf16[1,1,128,16,128]{4,3,2,1,0:T(8,128)(2,1)S(1)} %copy-done.9), channel_id=1, source_target_pairs={{0,2},{1,3},{2,0},{3,1},{4,6},{5,7},{6,4},{7,5},{8,10},{9,11},{10,... | collective-permute-start | bytes 1572872 | tf_op jit(solution)/shard_map/ppermute | solution.py:397
  10.2 34.8 %collective-permute-start.4 = (bf16[1,1,128,16,128]{4,3,2,1,0:T(8,128)(2,1)}, bf16[1,1,128,16,128]{4,3,2,1,0:T(8,128)(2,1)S(1)}, u32[]{:S(2)}, u32[]{:S(2)}) collective-permute-start(bf16[1,1,128,16,128]{4,3,2,1,0:T(8,128)(2,1)} %get-tuple-element.31), channel_id=1, source_target_pairs={{0,3},{1,2},{2,1},{3,0},{4,7},{5,6},{6,5},{7,4},{8,11},{9,10},{10,... | collective-permute-start | bytes 1572872 | tf_op jit(solution)/shard_map/ppermute | solution.py:397
  11.5 44.6 %collective-permute-start.6 = (bf16[1,1,128,16,128]{4,3,2,1,0:T(8,128)(2,1)S(1)}, bf16[1,1,128,16,128]{4,3,2,1,0:T(8,128)(2,1)S(1)}, u32[]{:S(2)}, u32[]{:S(2)}) collective-permute-start(bf16[1,1,128,16,128]{4,3,2,1,0:T(8,128)(2,1)S(1)} %copy-done.8), channel_id=1, source_target_pairs={{0,3},{1,2},{2,1},{3,0},{4,7},{5,6},{6,5},{7,4},{8,11},{9,10},{10,... | collective-permute-start | bytes 1572872 | tf_op jit(solution)/shard_map/ppermute | solution.py:397
  22.8 11.2 %copy-start.4 = (bf16[1,1,128,16,128]{4,3,2,1,0:T(8,128)(2,1)}, bf16[1,1,128,16,128]{4,3,2,1,0:T(8,128)(2,1)S(1)}, u32[]{:S(2)}) copy-start(bf16[1,1,128,16,128]{4,3,2,1,0:T(8,128)(2,1)S(1)} %collective-permute-done.5) | copy-start | bytes 1572868
  22.8 52.3 %collective-permute-start.8 = (bf16[1,1,128,16,128]{4,3,2,1,0:T(8,128)(2,1)}, bf16[1,1,128,16,128]{4,3,2,1,0:T(8,128)(2,1)S(1)}, u32[]{:S(2)}, u32[]{:S(2)}) collective-permute-start(bf16[1,1,128,16,128]{4,3,2,1,0:T(8,128)(2,1)} %get-tuple-element.38), channel_id=1, source_target_pairs={{0,2},{1,3},{2,0},{3,1},{4,6},{5,7},{6,4},{7,5},{8,10},{9,11},{10,... | collective-permute-start | bytes 1572872 | tf_op jit(solution)/shard_map/ppermute | solution.py:397
  34.1 37.3 %copy-start.3 = (bf16[1,1,128,16,128]{4,3,2,1,0:T(8,128)(2,1)}, bf16[1,1,128,16,128]{4,3,2,1,0:T(8,128)(2,1)S(1)}, u32[]{:S(2)}) copy-start(bf16[1,1,128,16,128]{4,3,2,1,0:T(8,128)(2,1)S(1)} %collective-permute-done.3) | copy-start | bytes 1572868
  34.1 44.6 %collective-permute-start.9 = (bf16[1,1,128,16,128]{4,3,2,1,0:T(8,128)(2,1)}, bf16[1,1,128,16,128]{4,3,2,1,0:T(8,128)(2,1)S(1)}, u32[]{:S(2)}, u32[]{:S(2)}) collective-permute-start(bf16[1,1,128,16,128]{4,3,2,1,0:T(8,128)(2,1)} %get-tuple-element.39), channel_id=1, source_target_pairs={{0,3},{1,2},{2,1},{3,0},{4,7},{5,6},{6,5},{7,4},{8,11},{9,10},{10,... | collective-permute-start | bytes 1572872 | tf_op jit(solution)/shard_map/ppermute | solution.py:397
  45.0 0.8 copy-start.5
  45.7 52.6 %collective-permute-start.1 = (bf16[1,1,128,16,128]{4,3,2,1,0:T(8,128)(2,1)S(1)}, bf16[1,1,128,16,128]{4,3,2,1,0:T(8,128)(2,1)S(1)}, u32[]{:S(2)}, u32[]{:S(2)}) collective-permute-start(bf16[1,1,128,16,128]{4,3,2,1,0:T(8,128)(2,1)S(1)} %copy-done.7), channel_id=1, source_target_pairs={{0,2},{1,3},{2,0},{3,1},{4,6},{5,7},{6,4},{7,5},{8,10},{9,11},{10,... | collective-permute-start | bytes 1572872 | tf_op jit(solution)/shard_map/ppermute | solution.py:397
  56.1 0.8 copy-start.6
  56.9 41.4 %collective-permute-start.2 = (bf16[1,1,96,16,128]{4,3,2,1,0:T(8,128)(2,1)}, bf16[1,1,96,16,128]{4,3,2,1,0:T(8,128)(2,1)S(1)}, u32[]{:S(2)}, u32[]{:S(2)}) collective-permute-start(bf16[1,1,96,16,128]{4,3,2,1,0:T(8,128)(2,1)} %get-tuple-element.29), channel_id=1, source_target_pairs={{0,3},{1,2},{2,1},{3,0},{4,7},{5,6},{6,5},{7,4},{8,11},{9,10},{10,... | collective-permute-start | bytes 1179656 | tf_op jit(solution)/shard_map/ppermute | solution.py:397
  59.5 41.4 %collective-permute-start = (bf16[1,1,32,16,128]{4,3,2,1,0:T(8,128)(2,1)}, bf16[1,1,32,16,128]{4,3,2,1,0:T(8,128)(2,1)S(1)}, u32[]{:S(2)}, u32[]{:S(2)}) collective-permute-start(bf16[1,1,32,16,128]{4,3,2,1,0:T(8,128)(2,1)} %get-tuple-element.27), channel_id=1, source_target_pairs={{0,3},{1,2},{2,1},{3,0},{4,7},{5,6},{6,5},{7,4},{8,11},{9,10},{10,... | collective-permute-start | bytes 393224 | tf_op jit(solution)/shard_map/ppermute | solution.py:397
  75.2 3.5 %copy-start.1 = (bf16[1,1,128,16,128]{4,3,2,1,0:T(8,128)(2,1)}, bf16[1,1,128,16,128]{4,3,2,1,0:T(8,128)(2,1)S(1)}, u32[]{:S(2)}) copy-start(bf16[1,1,128,16,128]{4,3,2,1,0:T(8,128)(2,1)S(1)} %collective-permute-done.8) | copy-start | bytes 1572868
  78.7 0.8 copy-start.2
